TPU v7x, 32 devices: a whole 2x2x4 slice. The times are simulated.
32 devices in a mesh: replica: 2 (over x), seq: 16 (over z, y, core).
Axes of the slice: x: 2, y: 2, z: 4, core: 2. Of those that a mesh axis runs over, the one named last changes fastest.
Arguments:
- hidden_in: bfloat16 [32, 8192], P('replica'), parts along dimension 0, may hold values from -6 to 6
- w_query: bfloat16 [8192, 8192], P(None, 'seq'), may hold values from -1 to 1
- w_keyval: bfloat16 [8192, 2048], P(None, 'seq'), may hold values from -0.1875 to 0.1875
- key_cache: bfloat16 [32, 2048, 1024], P('replica', 'seq'), parts along dimension 0, may hold values from -15 to 15
- value_cache: bfloat16 [32, 2048, 1024], P('replica', 'seq'), parts along dimension 0, may hold values from -6 to 6
- lengths: int32 [32], P('replica'), parts along dimension 0, may hold values from 128 to 2047, as said below
- w_out: bfloat16 [8192, 8192], P('seq'), may hold values from -0.09375 to 0.09375
Outputs:
- attn_out: bfloat16 [32, 8192], P('replica', 'seq'), parts along dimension 0
There are 2 independent parts, one for each index of `replica`. A program takes and returns all parts, laid end to end along the dimension named above; an argument that names none is the same for every part. Nothing has to cross between parts.
Inputs may be any that keep to these rules, and one draw needn't show every extreme that they name: The new token of sequence b is written at position lengths[b]; it attends to positions 0 to lengths[b].
All inputs are finite; a program needn't handle non-finite values.
Results may differ from a plain program's by a relative error of at most 0.013.
Values may be sent and summed in bfloat16 or wider, within the bound.
A program may use at most 64 MiB of HBM per device.

v0:
```python
import math

import jax
import jax.numpy as jnp
from jax import lax
from jax.sharding import PartitionSpec as P

KV_HEADS = 8
HEAD_DIM = 128


def regroup_merge(pieces):
    out_parts, max_parts, sum_parts = pieces
    largest = jnp.max(max_parts, axis=0)
    factor = jnp.exp(max_parts - largest[None])
    numerator = jnp.sum(out_parts * factor[..., None], axis=0)
    denominator = jnp.sum(sum_parts * factor, axis=0)
    return numerator / denominator[..., None]


def body(hidden_in, w_query, w_keyval, key_cache, value_cache, lengths, w_out):
    batch_rows, ctx_dev, half_width = key_cache.shape
    shards = lax.axis_size("seq")
    shard_index = lax.axis_index("seq")
    heads_dev = w_out.shape[0] // HEAD_DIM
    all_heads = heads_dev * shards
    group_size = all_heads // KV_HEADS
    query_part = jnp.dot(hidden_in, w_query, preferred_element_type=jnp.float32).astype(
        jnp.bfloat16
    )
    keyval_part = jnp.dot(hidden_in, w_keyval, preferred_element_type=jnp.float32).astype(
        jnp.bfloat16
    )
    query, new_kv = (
        lax.all_gather(query_part, "seq", axis=1, tiled=True),
        lax.all_gather(keyval_part, "seq", axis=1, tiled=True),
    )
    first_slot = shard_index * ctx_dev
    slot_ids = first_slot + lax.broadcasted_iota(jnp.int32, (batch_rows, ctx_dev), 1)
    is_new = (slot_ids == lengths[:, None])[..., None]
    key_rows = jnp.where(is_new, new_kv[:, None, :half_width], key_cache)
    value_rows = jnp.where(is_new, new_kv[:, None, half_width:], value_cache)
    grouped = query.reshape(batch_rows, KV_HEADS, group_size, HEAD_DIM)
    key_heads = key_rows.reshape(batch_rows, ctx_dev, KV_HEADS, HEAD_DIM)
    value_heads = value_rows.reshape(batch_rows, ctx_dev, KV_HEADS, HEAD_DIM)
    scores = jnp.einsum("bkgd,btkd->bkgt", grouped, key_heads, preferred_element_type=jnp.float32)
    scores = scores / math.sqrt(HEAD_DIM)
    used = (slot_ids <= lengths[:, None])[:, None, None, :]
    scores = jnp.where(used, scores, -1e30)
    local_max = jnp.max(scores, axis=-1)
    weights = jnp.exp(scores - local_max[..., None])
    local_sum = jnp.sum(weights, axis=-1)
    local_out = jnp.einsum(
        "bkgt,btkd->bkgd",
        weights.astype(jnp.bfloat16),
        value_heads,
        preferred_element_type=jnp.float32,
    )
    local_max = local_max.reshape(batch_rows, all_heads)
    local_sum = local_sum.reshape(batch_rows, all_heads)
    local_out = local_out.reshape(batch_rows, all_heads, HEAD_DIM)
    merged = regroup_merge(
        (
            lax.all_to_all(local_out[None], "seq", split_axis=2, concat_axis=0, tiled=True),
            lax.all_to_all(local_max[None], "seq", split_axis=2, concat_axis=0, tiled=True),
            lax.all_to_all(local_sum[None], "seq", split_axis=2, concat_axis=0, tiled=True),
        )
    )
    attended = merged.reshape(batch_rows, heads_dev * HEAD_DIM).astype(jnp.bfloat16)
    term = jnp.dot(attended, w_out, preferred_element_type=jnp.float32)
    return lax.psum_scatter(term, "seq", scatter_dimension=1, tiled=True).astype(jnp.bfloat16)


def solution(mesh):
    placed = (
        P("replica", None),
        P(None, "seq"),
        P(None, "seq"),
        P("replica", "seq", None),
        P("replica", "seq", None),
        P("replica"),
        P("seq", None),
    )
    return jax.shard_map(
        body, mesh=mesh, in_specs=placed, out_specs=P("replica", "seq"), check_vma=False
    )
```

profile of v0, /device:TPU:0, one launch (start us, length us, event | category | flops | bytes accessed | tf_op | source)
XLA Modules:
  0.0 169.5 jit_solution(1867745284692314005)
XLA Ops:
  6.5 0.0 copy-start
  6.5 1.6 copy-done
  8.1 1.3 convolution_convert_fusion.1
  9.5 0.0 copy-start.3
  9.5 0.0 copy-start.1
  9.5 0.0 copy-start.2
  9.5 4.8 %convolution_convert_fusion = bf16[16,512]{1,0:T(8,128)(2,1)S(1)} fusion(bf16[16,8192]{1,0:T(8,128)(2,1)} %param.7, bf16[8192,512]{1,0:T(8,128)(2,1)} %param.8), kind=kOutput, calls=%fused_computation.11 | convolution fusion | flops 134225920 | bytes 8667136 | tf_op jit(solution)/shard_map/dot_general | solution.py:28
  14.3 23.4 %all_gather.7 = bf16[16,2048]{1,0:T(8,128)(2,1)S(1)} all-gather(bf16[16,128]{1,0:T(8,128)(2,1)S(1)} %convolution_convert_fusion.1), channel_id=1, replica_groups=mesh['replica'=2,'seq'=16] {'seq'}, dimensions={1}, use_global_device_ids=true | all-gather | bytes 69632 | tf_op jit(solution)/shard_map/all_gather | solution.py:36
  37.7 18.1 %all_gather.6 = bf16[16,8192]{1,0:T(8,128)(2,1)S(1)} all-gather(bf16[16,512]{1,0:T(8,128)(2,1)S(1)} %convolution_convert_fusion), channel_id=1, replica_groups=mesh['replica'=2,'seq'=16] {'seq'}, dimensions={1}, use_global_device_ids=true | all-gather | bytes 278528 | tf_op jit(solution)/shard_map/all_gather | solution.py:35
  55.9 0.0 copy-done.3
  55.9 0.1 broadcast_compare_fusion.1
  56.0 0.0 copy-done.1
  56.0 0.0 copy-done.2
  56.0 2.3 %select_bitcast_fusion.1 = (bf16[16,16,8,8,128]{4,3,2,1,0:T(8,128)(2,1)S(1)}, bf16[16,16,8,8,128]{4,3,2,1,0:T(8,128)(2,1)}) fusion(bf16[16,128,1024]{2,1,0:T(8,128)(2,1)S(1)} %copy-done.1, pred[16,128]{1,0:T(8,128)(4,1)S(1)} %get-tuple-element.12, bf16[16,1024]{1,0:T(8,128)(2,1)S(1)} %get-tuple-element.7, bf16[16,128,1024]{2,1,0:T(8,128)(2,1)S(1)} %copy-done.2, ...), kind=kLoop, calls=%fused_computation.7 | loop fusion | flops 4194304 | bytes 16844800
  58.3 2.3 %fusion.24 = (f32[16,8,8]{2,1,0:T(8,128)S(1)}, f32[16,8,8,128]{3,2,1,0:T(8,128)S(1)}) fusion(bf16[16,8,8,128]{3,2,1,0:T(8,128)(2,1)S(1)} %bitcast.58, bf16[16,16,8,8,128]{4,3,2,1,0:T(8,128)(2,1)S(1)} %get-tuple-element.9, pred[16,128]{1,0:T(8,128)(4,1)S(1)} %get-tuple-element.11), kind=kOutput, calls=%fused_computation.29 | convolution fusion | flops 33946624 | bytes 4986880 | tf_op jit(solution)/shard_map/bkgd,btkd->bkgt/dot_general | solution.py:46
  60.6 0.7 copy.32
  61.4 3.5 %all-to-all-start.1 = ((f32[1,16,64]{1,0,2:T(1,128)}), f32[1,16,64]{1,0,2:T(1,128)S(1)}, u32[]{:S(2)}, u32[]{:S(2)}) async-start(f32[1,16,64]{1,0,2:T(1,128)} %bitcast.5), calls=%async_computation.1 | async-start | bytes 65536 | tf_op jit(solution)/shard_map/all_to_all | solution.py:65
  64.9 0.4 fusion.15
  65.3 0.7 copy.34
  66.0 5.5 %all-to-all-done.1 = f32[1,16,64]{1,0,2:T(1,128)S(1)} async-done(((f32[1,16,64]{1,0,2:T(1,128)}), f32[1,16,64]{1,0,2:T(1,128)S(1)}, u32[]{:S(2)}, u32[]{:S(2)}) %all-to-all-start.1) | async-done | bytes 4128 | tf_op jit(solution)/shard_map/all_to_all | solution.py:65
  71.5 3.5 %all-to-all-start.2 = ((f32[1,16,64]{1,0,2:T(1,128)}), f32[1,16,64]{1,0,2:T(1,128)S(1)}, u32[]{:S(2)}, u32[]{:S(2)}) async-start(f32[1,16,64]{1,0,2:T(1,128)} %bitcast.11), calls=%async_computation.2 | async-start | bytes 65536 | tf_op jit(solution)/shard_map/all_to_all | solution.py:66
  74.9 3.4 %fusion.6 = f32[1,16,64,128]{3,2,1,0:T(8,128)S(1)} fusion(bf16[16,16,8,8,128]{4,3,2,1,0:T(8,128)(2,1)} %get-tuple-element.10, f32[16,8,8,128]{3,2,1,0:T(8,128)S(1)} %get-tuple-element.14, f32[16,8,8]{2,1,0:T(8,128)S(1)} %get-tuple-element.13), kind=kOutput, calls=%fused_computation.8 | convolution fusion | flops 33816576 | bytes 5246976 | tf_op jit(solution)/shard_map/bkgt,btkd->bkgd/dot_general | solution.py:53
  78.4 1.1 copy.31
  79.5 2.1 %all-to-all-done.2 = f32[1,16,64]{1,0,2:T(1,128)S(1)} async-done(((f32[1,16,64]{1,0,2:T(1,128)}), f32[1,16,64]{1,0,2:T(1,128)S(1)}, u32[]{:S(2)}, u32[]{:S(2)}) %all-to-all-start.2) | async-done | bytes 4128 | tf_op jit(solution)/shard_map/all_to_all | solution.py:66
  81.5 3.9 %all-to-all-start = ((f32[1,16,64,128]{3,1,0,2:T(8,128)}), f32[1,16,64,128]{3,1,0,2:T(8,128)S(1)}, u32[]{:S(2)}, u32[]{:S(2)}) async-start(f32[1,16,64,128]{3,1,0,2:T(8,128)} %copy.31), calls=%async_computation | async-start | bytes 1048576 | tf_op jit(solution)/shard_map/all_to_all | solution.py:64
  85.5 0.0 reduce-scatter.2.cloned.1.call-start
  85.6 14.2 %all-to-all-done = f32[1,16,64,128]{3,1,0,2:T(8,128)S(1)} async-done(((f32[1,16,64,128]{3,1,0,2:T(8,128)}), f32[1,16,64,128]{3,1,0,2:T(8,128)S(1)}, u32[]{:S(2)}, u32[]{:S(2)}) %all-to-all-start) | async-done | bytes 524320 | tf_op jit(solution)/shard_map/all_to_all | solution.py:64
  99.7 0.2 multiply_reduce_fusion
  99.9 5.4 %fusion.19 = f32[16,8192]{1,0:T(8,128)} fusion(bf16[512,8192]{1,0:T(8,128)(2,1)} %param.13, f32[16,4,128]{2,0,1:T(8,128)S(1)} %multiply_reduce_fusion, f32[16,4]{0,1:T(4,128)S(1)} %get-tuple-element.5), kind=kOutput, calls=%fused_computation.21 | convolution fusion | flops 134234112 | bytes 8945920 | tf_op jit(solution)/shard_map/dot_general | solution.py:70
  105.4 0.0 reduce-scatter.2.cloned.1.call-update
  105.4 55.9 %reduce-scatter.2.cloned.1.call-done = f32[16,512]{1,0:T(8,128)} async-done(((f32[16,8192]{1,0:T(8,128)}), f32[16,512]{1,0:T(8,128)}) %reduce-scatter.2.cloned.1.call-update) | async-done | bytes 32784 | tf_op jit(solution)/shard_map/reduce_scatter | solution.py:71
  161.3 1.4 convert_element_type.23
  (5 shorter events, 0.1 us)
Async XLA Ops:
  6.5 1.6 copy-start
  9.5 46.4 %copy-start.3 = (s32[16]{0:T(128)S(1)}, s32[16]{0:T(128)}, u32[]{:S(2)}) copy-start(s32[16]{0:T(128)} %param.12) | copy-start | bytes 196
  9.5 46.5 %copy-start.1 = (bf16[16,128,1024]{2,1,0:T(8,128)(2,1)S(1)}, bf16[16,128,1024]{2,1,0:T(8,128)(2,1)}, u32[]{:S(2)}) copy-start(bf16[16,128,1024]{2,1,0:T(8,128)(2,1)} %param.10) | copy-start | bytes 12582916
  9.5 46.5 %copy-start.2 = (bf16[16,128,1024]{2,1,0:T(8,128)(2,1)S(1)}, bf16[16,128,1024]{2,1,0:T(8,128)(2,1)}, u32[]{:S(2)}) copy-start(bf16[16,128,1024]{2,1,0:T(8,128)(2,1)} %param.11) | copy-start | bytes 12582916
  61.4 10.1 %all-to-all-start.1 = ((f32[1,16,64]{1,0,2:T(1,128)}), f32[1,16,64]{1,0,2:T(1,128)S(1)}, u32[]{:S(2)}, u32[]{:S(2)}) async-start(f32[1,16,64]{1,0,2:T(1,128)} %bitcast.5), calls=%async_computation.1 | async-start | bytes 65536 | tf_op jit(solution)/shard_map/all_to_all | solution.py:65
  71.5 10.1 %all-to-all-start.2 = ((f32[1,16,64]{1,0,2:T(1,128)}), f32[1,16,64]{1,0,2:T(1,128)S(1)}, u32[]{:S(2)}, u32[]{:S(2)}) async-start(f32[1,16,64]{1,0,2:T(1,128)} %bitcast.11), calls=%async_computation.2 | async-start | bytes 65536 | tf_op jit(solution)/shard_map/all_to_all | solution.py:66
  81.5 18.2 %all-to-all-start = ((f32[1,16,64,128]{3,1,0,2:T(8,128)}), f32[1,16,64,128]{3,1,0,2:T(8,128)S(1)}, u32[]{:S(2)}, u32[]{:S(2)}) async-start(f32[1,16,64,128]{3,1,0,2:T(8,128)} %copy.31), calls=%async_computation | async-start | bytes 1048576 | tf_op jit(solution)/shard_map/all_to_all | solution.py:64
  85.5 75.8 %reduce-scatter.2.cloned.1.call-start = ((), (), s32[]{:S(2)}) async-start(), calls=%async_computation.4 | async-start | bytes 557056 | tf_op jit(solution)/shard_map/reduce_scatter | solution.py:71
Sparse Core Ops, SparseCore 0:
  105.5 55.7 reduce-scatter.1
where the time goes:
time: 170 us; the launch traced here: 169 us
  waiting for transfers between devices  77.6 us (46%)
  blocking collectives  41.5 us (24%)
  matrix products  17.3 us (10%)
  between operations  13.5 us (8%)
  starting transfers between devices  10.9 us (6%)
  other arithmetic  4.43 us (3%)
  local copies, waits for them, and re-layouts  4.2 us (2%)
    reduce_scatter x1, waiting for transfers between devices, body(): lax.psum_scatter(term, 'seq', scatter_dimension=1, tiled=True)  55.9 us
    all_gather x1, blocking collectives, body(): lax.all_gather(keyval_part, 'seq', axis=1, tiled=True)  23.4 us
    all_gather x1, blocking collectives, body(): lax.all_gather(query_part, 'seq', axis=1, tiled=True)  18.1 us
    all_to_all x1, waiting for transfers between devices, body(): lax.all_to_all(local_out[None], 'seq', split_axis=2, concat_axis=0, tiled...  14.2 us
    all_to_all x1, waiting for transfers between devices, body(): lax.all_to_all(local_max[None], 'seq', split_axis=2, concat_axis=0, tiled...  5.47 us
    dot_general x1, matrix products, body(): term = jnp.dot(attended, w_out, preferred_element_type=jnp.float32)  5.42 us
    dot_general x1, matrix products, body(): jnp.dot(hidden_in, w_query, preferred_element_type=jnp.float32)  4.79 us
    all_to_all x1, starting transfers between devices, body(): lax.all_to_all(local_out[None], 'seq', split_axis=2, concat_axis=0, tiled...  3.92 us
  transfers between devices with their start and end apart: 4, of which 4 were waited for; matrix products, arithmetic and copies ran while one was open for 3% of the time, Pallas kernels for 0%

commit v1 on v0

v1 whole, which is shorter than its diff:
```python
import functools
import math

import jax
import jax.numpy as jnp
from jax import lax
from jax.experimental import pallas as pl
from jax.experimental.pallas import tpu as pltpu
from jax.sharding import PartitionSpec as P

KV_HEADS = 8
HEAD_DIM = 128
LANES = 128
MESH = pl.DeviceIdType.MESH
F32 = jnp.float32
BF16 = jnp.bfloat16


def kernel(
    shards, chunks,
    x_hbm, wq_hbm, wkv_hbm, kc_hbm, vc_hbm, len_ref, wo_hbm,
    out_ref,
    x_v, wq_v, wkv_v, kc_v, vc_v, wo_v,
    q_all, kv_s, kv_r, qf, of, lf, part_s, part_r, att_v, term_s, term_r,
    x_sem, wq_sem, wkv_sem, kc_sem, vc_sem, wo_sem,
    q_send, q_recv, kv_send, kv_recv, p_send, p_recv, t_send, t_recv,
):
    me = lax.axis_index("seq")
    batch, ctx_dev = kc_v.shape[0], kc_v.shape[1]
    depth = x_v.shape[1]
    width = q_all.shape[2]
    heads_dev = width // HEAD_DIM
    owners = shards // KV_HEADS
    group = owners * heads_dev
    kv_cols = kv_s.shape[1]
    pieces = HEAD_DIM // kv_cols
    step = depth // chunks
    region = LANES // heads_dev

    x_copy = pltpu.make_async_copy(x_hbm, x_v, x_sem)
    x_copy.start()
    wq_copies, wkv_copies = [], []
    for c in range(chunks):
        rows = pl.ds(c * step, step)
        wq_copies.append(pltpu.make_async_copy(wq_hbm.at[rows], wq_v.at[rows], wq_sem.at[c]))
        wkv_copies.append(pltpu.make_async_copy(wkv_hbm.at[rows], wkv_v.at[rows], wkv_sem.at[c]))
        wq_copies[c].start()
        wkv_copies[c].start()
    kc_copy = pltpu.make_async_copy(kc_hbm, kc_v, kc_sem)
    vc_copy = pltpu.make_async_copy(vc_hbm, vc_v, vc_sem)
    wo_copy = pltpu.make_async_copy(wo_hbm, wo_v, wo_sem)

    barrier = pltpu.get_barrier_semaphore()

    def greet(i, carry):
        pl.semaphore_signal(
            barrier, inc=1, device_id={"seq": lax.rem(me + i, shards)}, device_id_type=MESH
        )
        return carry

    lax.fori_loop(1, shards, greet, 0)

    acc_q = jnp.zeros((batch, width), F32)
    acc_kv = jnp.zeros((batch, kv_cols), F32)
    x_copy.wait()
    for c in range(chunks):
        wq_copies[c].wait()
        wkv_copies[c].wait()
        part = x_v[:, c * step:(c + 1) * step]
        acc_q += jnp.dot(part, wq_v[c * step:(c + 1) * step, :], preferred_element_type=F32)
        acc_kv += jnp.dot(part, wkv_v[c * step:(c + 1) * step, :], preferred_element_type=F32)
        if c == chunks // 2:
            kc_copy.start()
            vc_copy.start()
            wo_copy.start()
    q_all[me] = acc_q.astype(BF16)
    kv_s[...] = acc_kv.astype(BF16)

    pl.semaphore_wait(barrier, shards - 1)

    def q_copy(slot, peer):
        return pltpu.make_async_remote_copy(
            src_ref=q_all.at[slot], dst_ref=q_all.at[slot],
            send_sem=q_send.at[peer], recv_sem=q_recv.at[slot],
            device_id={"seq": peer}, device_id_type=MESH,
        )

    def send_q(i, carry):
        q_copy(me, lax.rem(me + i, shards)).start()
        return carry

    lax.fori_loop(1, shards, send_q, 0)

    half = shards // 2
    role = me // half
    within = me - role * half
    my_head = within // pieces
    my_slot = role * pieces + (within - my_head * pieces)

    def kv_copy(slot, peer, g):
        return pltpu.make_async_remote_copy(
            src_ref=kv_s, dst_ref=kv_r.at[slot],
            send_sem=kv_send.at[g], recv_sem=kv_recv.at[slot],
            device_id={"seq": peer}, device_id_type=MESH,
        )

    def kv_local():
        return pltpu.make_async_copy(kv_s, kv_r.at[my_slot], kv_recv.at[my_slot])

    for g in range(owners):
        peer = my_head * owners + g

        @pl.when(peer != me)
        def _():
            kv_copy(my_slot, peer, g).start()

        @pl.when(peer == me)
        def _():
            kv_local().start()

    kc_copy.wait()
    vc_copy.wait()

    first = me * ctx_dev
    scale = 1.0 / math.sqrt(HEAD_DIM)
    my_group = me // owners
    slots = lax.broadcasted_iota(jnp.int32, (group, ctx_dev), 1) + first
    lane = lax.broadcasted_iota(jnp.int32, (batch, LANES), 1)

    def part_copy(src_slot, dst_slot, peer):
        return pltpu.make_async_remote_copy(
            src_ref=part_s.at[src_slot], dst_ref=part_r.at[dst_slot],
            send_sem=p_send.at[peer], recv_sem=p_recv.at[dst_slot],
            device_id={"seq": peer}, device_id_type=MESH,
        )

    def part_local():
        return pltpu.make_async_copy(part_s.at[me], part_r.at[me], p_recv.at[me])

    def attend(i, carry):
        k = lax.rem(my_group + i, KV_HEADS)
        cols = pl.ds(pl.multiple_of(k * HEAD_DIM, HEAD_DIM), HEAD_DIM)
        for g in range(owners):
            src = k * owners + g

            @pl.when(src != me)
            def _():
                q_copy(src, src).wait_recv()

        for g in range(owners):
            block = q_all[k * owners + g].astype(F32)
            for h in range(heads_dev):
                qf[:, g * heads_dev + h, :] = block[:, h * HEAD_DIM:(h + 1) * HEAD_DIM]
        for b in range(batch):
            scores = lax.dot_general(
                qf[b].astype(BF16), kc_v[b, :, cols], (((1,), (1,)), ((), ())),
                preferred_element_type=F32,
            ) * scale
            scores = jnp.where(slots < len_ref[b], scores, -1e30)
            largest = jnp.max(scores, axis=-1, keepdims=True)
            weights = jnp.exp(scores - largest)
            total = jnp.sum(weights, axis=-1, keepdims=True)
            summed = jnp.dot(weights.astype(BF16), vc_v[b, :, cols], preferred_element_type=F32)
            of[b] = summed / total
            lf[b] = jnp.broadcast_to(largest + jnp.log(total), (group, LANES))
        for g in range(owners):
            d = k * owners + g
            stats = jnp.zeros((batch, LANES), F32)
            for h in range(heads_dev):
                part_s[d, :, h * HEAD_DIM:(h + 1) * HEAD_DIM] = of[:, g * heads_dev + h, :].astype(BF16)
                lse = lf[:, g * heads_dev + h, :]
                high = lse.astype(BF16).astype(F32)
                mid = (lse - high).astype(BF16).astype(F32)
                low = lse - high - mid
                base = h * region
                stats = jnp.where(lane == base, high, stats)
                stats = jnp.where(lane == base + 1, mid, stats)
                stats = jnp.where(lane == base + 2, low, stats)
            part_s[d, :, width:] = stats.astype(BF16)

            @pl.when(d != me)
            def _():
                part_copy(d, me, d).start()

            @pl.when(d == me)
            def _():
                part_local().start()

        return carry

    lax.fori_loop(0, KV_HEADS, attend, 0)

    owner_head = me // owners
    for r in range(2 * pieces):
        src = (r // pieces) * half + owner_head * pieces + r % pieces

        @pl.when(src != me)
        def _():
            kv_copy(r, src, 0).wait_recv()

        @pl.when(src == me)
        def _():
            kv_local().wait()

    def wait_part(i, carry):
        part_copy(lax.rem(me + i, shards), lax.rem(me + i, shards), lax.rem(me + i, shards)).wait_recv()
        return carry

    lax.fori_loop(1, shards, wait_part, 0)
    part_local().wait()

    def lse_of(s, h):
        stats = part_r[s, :, width:].astype(F32)
        mine = (lane >= h * region) & (lane < (h + 1) * region)
        return jnp.sum(jnp.where(mine, stats, 0.0), axis=-1, keepdims=True)

    new_value = jnp.concatenate([kv_r[pieces + p].astype(F32) for p in range(pieces)], axis=-1)
    new_key = jnp.concatenate([kv_r[p].astype(F32) for p in range(pieces)], axis=-1)
    own_q = q_all[me].astype(F32)
    fresh = [
        jnp.sum(own_q[:, h * HEAD_DIM:(h + 1) * HEAD_DIM] * new_key, axis=-1, keepdims=True) * scale
        for h in range(heads_dev)
    ]

    def top_of(s, tops):
        return tuple(jnp.maximum(t, lse_of(s, h)) for h, t in enumerate(tops))

    tops = lax.fori_loop(0, shards, top_of, tuple(fresh))
    shares = [jnp.exp(f - t) for f, t in zip(fresh, tops)]

    def merge(s, state):
        sums, totals = state
        new_sums, new_totals = [], []
        for h in range(heads_dev):
            share = jnp.exp(lse_of(s, h) - tops[h])
            values = part_r[s, :, h * HEAD_DIM:(h + 1) * HEAD_DIM].astype(F32)
            new_sums.append(sums[h] + share * values)
            new_totals.append(totals[h] + share)
        return tuple(new_sums), tuple(new_totals)

    sums, totals = lax.fori_loop(
        0, shards, merge, (tuple(s * new_value for s in shares), tuple(shares))
    )
    for h in range(heads_dev):
        att_v[:, h * HEAD_DIM:(h + 1) * HEAD_DIM] = (sums[h] / totals[h]).astype(BF16)

    wo_copy.wait()
    out_cols = term_s.shape[2]

    def term_copy(src_slot, dst_slot, peer):
        return pltpu.make_async_remote_copy(
            src_ref=term_s.at[src_slot], dst_ref=term_r.at[dst_slot],
            send_sem=t_send.at[peer], recv_sem=t_recv.at[dst_slot],
            device_id={"seq": peer}, device_id_type=MESH,
        )

    def term_of(d):
        cols = pl.ds(pl.multiple_of(d * out_cols, out_cols), out_cols)
        return jnp.dot(att_v[...], wo_v[:, cols], preferred_element_type=F32)

    def project(i, carry):
        d = lax.rem(me + i, shards)
        term_s[d] = term_of(d).astype(BF16)
        term_copy(d, me, d).start()
        return carry

    lax.fori_loop(1, shards, project, 0)
    own = term_of(me)

    def collect(i, total):
        s = lax.rem(me + i, shards)
        term_copy(s, s, s).wait_recv()
        return total + term_r[s].astype(F32)

    out_ref[...] = lax.fori_loop(1, shards, collect, own).astype(BF16)

    def drain(i, carry):
        peer = lax.rem(me + i, shards)
        q_copy(me, peer).wait_send()
        part_copy(peer, peer, peer).wait_send()
        term_copy(peer, peer, peer).wait_send()
        return carry

    lax.fori_loop(1, shards, drain, 0)
    for g in range(owners):
        peer = my_head * owners + g

        @pl.when(peer != me)
        def _():
            kv_copy(my_slot, peer, g).wait_send()


def body(hidden_in, w_query, w_keyval, key_cache, value_cache, lengths, w_out):
    shards = lax.axis_size("seq")
    batch, depth = hidden_in.shape
    width = w_query.shape[1]
    kv_cols = w_keyval.shape[1]
    heads_dev = width // HEAD_DIM
    owners = shards // KV_HEADS
    group = owners * heads_dev
    pieces = HEAD_DIM // kv_cols
    out_cols = w_out.shape[1] // shards
    chunks = 8
    dma = pltpu.SemaphoreType.DMA
    hbm = pl.BlockSpec(memory_space=pl.ANY)
    return pl.pallas_call(
        functools.partial(kernel, shards, chunks),
        out_shape=jax.ShapeDtypeStruct((batch, out_cols), BF16),
        in_specs=[hbm, hbm, hbm, hbm, hbm, pl.BlockSpec(memory_space=pltpu.SMEM), hbm],
        out_specs=pl.BlockSpec(memory_space=pltpu.VMEM),
        scratch_shapes=[
            pltpu.VMEM(hidden_in.shape, BF16),
            pltpu.VMEM(w_query.shape, BF16),
            pltpu.VMEM(w_keyval.shape, BF16),
            pltpu.VMEM(key_cache.shape, BF16),
            pltpu.VMEM(value_cache.shape, BF16),
            pltpu.VMEM(w_out.shape, BF16),
            pltpu.VMEM((shards, batch, width), BF16),
            pltpu.VMEM((batch, kv_cols), BF16),
            pltpu.VMEM((2 * pieces, batch, kv_cols), BF16),
            pltpu.VMEM((batch, group, HEAD_DIM), F32),
            pltpu.VMEM((batch, group, HEAD_DIM), F32),
            pltpu.VMEM((batch, group, LANES), F32),
            pltpu.VMEM((shards, batch, width + LANES), BF16),
            pltpu.VMEM((shards, batch, width + LANES), BF16),
            pltpu.VMEM((batch, width), BF16),
            pltpu.VMEM((shards, batch, out_cols), BF16),
            pltpu.VMEM((shards, batch, out_cols), BF16),
            dma, dma((chunks,)), dma((chunks,)), dma, dma, dma,
            dma((shards,)), dma((shards,)), dma((owners,)), dma((2 * pieces,)),
            dma((shards,)), dma((shards,)), dma((shards,)), dma((shards,)),
        ],
        compiler_params=pltpu.CompilerParams(
            collective_id=0, has_side_effects=True, vmem_limit_bytes=60 * 1024 * 1024
        ),
    )(hidden_in, w_query, w_keyval, key_cache, value_cache, lengths, w_out)


def solution(mesh):
    placed = (
        P("replica", None),
        P(None, "seq"),
        P(None, "seq"),
        P("replica", "seq", None),
        P("replica", "seq", None),
        P("replica"),
        P("seq", None),
    )
    return jax.shard_map(
        body, mesh=mesh, in_specs=placed, out_specs=P("replica", "seq"), check_vma=False
    )
```

time: 170 us -> 60.2 us (0.35)
  waiting for transfers between devices: 77.6 us -> 0 us
  Pallas kernels: 0 us -> 58.5 us
  blocking collectives: 41.5 us -> 0 us
  matrix products: 17.3 us -> 0 us
  between operations: 13.5 us -> 0.01 us
  starting transfers between devices: 10.9 us -> 0 us
  other arithmetic: 4.43 us -> 0 us
  local copies, waits for them, and re-layouts: 4.2 us -> 1.32 us
    pallas_call x0 -> x1, Pallas kernels: none -> 58.5 us  [body(): pl.pallas_call(functools.partial(kernel, shards, chunks), out_shape=jax.S...]
    reduce_scatter x1 -> x0, waiting for transfers between devices: 55.9 us -> none  [body(): lax.psum_scatter(term, 'seq', scatter_dimension=1, tiled=True)]
    all_gather x2 -> x0, blocking collectives: 41.5 us -> none  [the longest x1 23.4 us: body(): lax.all_gather(keyval_part, 'seq', axis=1, tiled=True)]
    all_to_all x3 -> x0, waiting for transfers between devices: 21.7 us -> none  [the longest x1 14.2 us: body(): lax.all_to_all(local_out[None], 'seq', split_axis=2, concat_axis=0, tiled...]
    dot_general x5 -> x0, matrix products: 17.3 us -> none  [the longest x1 5.42 us: body(): term = jnp.dot(attended, w_out, preferred_element_type=jnp.float32)]
    all_to_all x3 -> x0, starting transfers between devices: 10.9 us -> none  [the longest x1 3.92 us: body(): lax.all_to_all(local_out[None], 'seq', split_axis=2, concat_axis=0, tiled...]
    unnamed x1 -> x0, other arithmetic: 2.32 us -> none
  transfers between devices with their start and end apart: 4 -> 0, of which waited for: 4 -> 0; matrix products, arithmetic and copies ran while one was open for 3% -> 0% of each run, Pallas kernels for 0% -> 0%
where the time goes in v1:
time: 60.2 us; the launch traced here: 59.8 us
  Pallas kernels  58.5 us (97%)
  local copies, waits for them, and re-layouts  1.32 us (2%)
    pallas_call x1, Pallas kernels, body(): pl.pallas_call(functools.partial(kernel, shards, chunks), out_shape=jax.S...  58.5 us
    unnamed x1, local copies, waits for them, and re-layouts  1.32 us

profile of v1, /device:TPU:0, one launch (start us, length us, event | category | flops | bytes accessed | tf_op | source)
XLA Modules:
  0.0 59.8 jit_solution(1533069464831637179)
XLA Ops:
  0.0 58.5 %shard_map.73 = bf16[16,512]{1,0:T(8,128)(2,1)} custom-call(bf16[16,8192]{1,0:T(8,128)(2,1)} %x_hbm.1, bf16[8192,512]{1,0:T(8,128)(2,1)} %wq_hbm.1, bf16[8192,128]{1,0:T(8,128)(2,1)} %wkv_hbm.1, bf16[16,128,1024]{2,1,0:T(8,128)(2,1)} %kc_hbm.1, bf16[16,128,1024]{2,1,0:T(8,128)(2,1)} %vc_hbm.1, s32[16]{0:T(128)} %len_ref.1, bf16[512,8192]{1,0:T(8,128)(2,1)} %wo_hbm.1), custom_call_target="tpu_custom_call" | custom-call | tf_op jit(solution)/shard_map/pallas_call | solution.py:306
  58.5 1.3 %copy.9 = bf16[16,512]{1,0:T(8,128)(2,1)} copy(bf16[16,512]{1,0:T(8,128)(2,1)} %shard_map.73) | data formatting | bytes 32768

commit v2 on v1

--- a/solution.py
+++ b/solution.py
@@ -11,6 +11,7 @@
 KV_HEADS = 8
 HEAD_DIM = 128
 LANES = 128
+PAIR = 2
 MESH = pl.DeviceIdType.MESH
 F32 = jnp.float32
 BF16 = jnp.bfloat16
@@ -124,7 +125,9 @@
     first = me * ctx_dev
     scale = 1.0 / math.sqrt(HEAD_DIM)
     my_group = me // owners
-    slots = lax.broadcasted_iota(jnp.int32, (group, ctx_dev), 1) + first
+    slots = lax.broadcasted_iota(jnp.int32, (PAIR * group, ctx_dev), 1) + first
+    used = jnp.stack([slots < len_ref[b] for b in range(batch)])
+    row_head = lax.broadcasted_iota(jnp.int32, (PAIR * group, HEAD_DIM), 0) // group
     lane = lax.broadcasted_iota(jnp.int32, (batch, LANES), 1)
 
     def part_copy(src_slot, dst_slot, peer):
@@ -138,33 +141,50 @@
         return pltpu.make_async_copy(part_s.at[me], part_r.at[me], p_recv.at[me])
 
     def attend(i, carry):
-        k = lax.rem(my_group + i, KV_HEADS)
-        cols = pl.ds(pl.multiple_of(k * HEAD_DIM, HEAD_DIM), HEAD_DIM)
-        for g in range(owners):
-            src = k * owners + g
+        pair = lax.rem(my_group // PAIR + i, KV_HEADS // PAIR)
+        cols = pl.ds(pl.multiple_of(pair * PAIR * HEAD_DIM, PAIR * HEAD_DIM), PAIR * HEAD_DIM)
+        devices = PAIR * owners
+
+        def wait_q(g, c):
+            src = pair * devices + g
 
             @pl.when(src != me)
             def _():
                 q_copy(src, src).wait_recv()
 
-        for g in range(owners):
-            block = q_all[k * owners + g].astype(F32)
+            return c
+
+        lax.fori_loop(0, devices, wait_q, 0)
+        for g in range(devices):
+            block = q_all[pair * devices + g].astype(F32)
             for h in range(heads_dev):
                 qf[:, g * heads_dev + h, :] = block[:, h * HEAD_DIM:(h + 1) * HEAD_DIM]
+        scores = []
         for b in range(batch):
-            scores = lax.dot_general(
-                qf[b].astype(BF16), kc_v[b, :, cols], (((1,), (1,)), ((), ())),
+            rows = qf[b]
+            wide = jnp.concatenate(
+                [jnp.where(row_head == n, rows, 0.0) for n in range(PAIR)], axis=1
+            )
+            scores.append(lax.dot_general(
+                wide.astype(BF16), kc_v[b, :, cols], (((1,), (1,)), ((), ())),
                 preferred_element_type=F32,
-            ) * scale
-            scores = jnp.where(slots < len_ref[b], scores, -1e30)
-            largest = jnp.max(scores, axis=-1, keepdims=True)
-            weights = jnp.exp(scores - largest)
-            total = jnp.sum(weights, axis=-1, keepdims=True)
-            summed = jnp.dot(weights.astype(BF16), vc_v[b, :, cols], preferred_element_type=F32)
-            of[b] = summed / total
-            lf[b] = jnp.broadcast_to(largest + jnp.log(total), (group, LANES))
-        for g in range(owners):
-            d = k * owners + g
+            ))
+        scores = jnp.where(used, jnp.stack(scores) * scale, -1e30)
+        largest = jnp.max(scores, axis=-1, keepdims=True)
+        weights = jnp.exp(scores - largest)
+        total = jnp.sum(weights, axis=-1, keepdims=True)
+        lf[...] = jnp.broadcast_to(largest + jnp.log(total), lf.shape)
+        inverse = 1.0 / total
+        weights = weights.astype(BF16)
+        for b in range(batch):
+            summed = jnp.dot(weights[b], vc_v[b, :, cols], preferred_element_type=F32)
+            mine = [
+                summed[n * group:(n + 1) * group, n * HEAD_DIM:(n + 1) * HEAD_DIM]
+                for n in range(PAIR)
+            ]
+            of[b] = jnp.concatenate(mine, axis=0) * inverse[b]
+        for g in range(devices):
+            d = pair * devices + g
             stats = jnp.zeros((batch, LANES), F32)
             for h in range(heads_dev):
                 part_s[d, :, h * HEAD_DIM:(h + 1) * HEAD_DIM] = of[:, g * heads_dev + h, :].astype(BF16)
@@ -178,6 +198,9 @@
                 stats = jnp.where(lane == base + 2, low, stats)
             part_s[d, :, width:] = stats.astype(BF16)
 
+        def send_part(g, c):
+            d = pair * devices + g
+
             @pl.when(d != me)
             def _():
                 part_copy(d, me, d).start()
@@ -186,9 +209,12 @@
             def _():
                 part_local().start()
 
-        return carry
-
-    lax.fori_loop(0, KV_HEADS, attend, 0)
+            return c
+
+        lax.fori_loop(0, devices, send_part, 0)
+        return carry
+
+    lax.fori_loop(0, KV_HEADS // PAIR, attend, 0)
 
     owner_head = me // owners
     for r in range(2 * pieces):
@@ -318,9 +344,9 @@
             pltpu.VMEM((shards, batch, width), BF16),
             pltpu.VMEM((batch, kv_cols), BF16),
             pltpu.VMEM((2 * pieces, batch, kv_cols), BF16),
-            pltpu.VMEM((batch, group, HEAD_DIM), F32),
-            pltpu.VMEM((batch, group, HEAD_DIM), F32),
-            pltpu.VMEM((batch, group, LANES), F32),
+            pltpu.VMEM((batch, PAIR * group, HEAD_DIM), F32),
+            pltpu.VMEM((batch, PAIR * group, HEAD_DIM), F32),
+            pltpu.VMEM((batch, PAIR * group, LANES), F32),
             pltpu.VMEM((shards, batch, width + LANES), BF16),
             pltpu.VMEM((shards, batch, width + LANES), BF16),
             pltpu.VMEM((batch, width), BF16),

time: 60.2 us -> 38.9 us (0.65)
  Pallas kernels: 58.5 us -> 37.3 us
    pallas_call x1, Pallas kernels: 58.5 us -> 37.3 us  [body(): pl.pallas_call(functools.partial(kernel, shards, chunks), out_shape=jax.S...]
where the time goes in v2:
time: 38.9 us; the launch traced here: 38.7 us
  Pallas kernels  37.3 us (96%)
  local copies, waits for them, and re-layouts  1.32 us (3%)
    pallas_call x1, Pallas kernels, body(): pl.pallas_call(functools.partial(kernel, shards, chunks), out_shape=jax.S...  37.3 us
    unnamed x1, local copies, waits for them, and re-layouts  1.32 us

profile of v2, /device:TPU:0, one launch (start us, length us, event | category | flops | bytes accessed | tf_op | source)
XLA Modules:
  0.0 38.7 jit_solution(7849984311883022457)
XLA Ops:
  0.0 37.3 %shard_map.73 = bf16[16,512]{1,0:T(8,128)(2,1)} custom-call(bf16[16,8192]{1,0:T(8,128)(2,1)} %x_hbm.1, bf16[8192,512]{1,0:T(8,128)(2,1)} %wq_hbm.1, bf16[8192,128]{1,0:T(8,128)(2,1)} %wkv_hbm.1, bf16[16,128,1024]{2,1,0:T(8,128)(2,1)} %kc_hbm.1, bf16[16,128,1024]{2,1,0:T(8,128)(2,1)} %vc_hbm.1, s32[16]{0:T(128)} %len_ref.1, bf16[512,8192]{1,0:T(8,128)(2,1)} %wo_hbm.1), custom_call_target="tpu_custom_call" | custom-call | tf_op jit(solution)/shard_map/pallas_call | solution.py:332
  37.3 1.3 %copy.9 = bf16[16,512]{1,0:T(8,128)(2,1)} copy(bf16[16,512]{1,0:T(8,128)(2,1)} %shard_map.73) | data formatting | bytes 32768

commit v3 on v2

--- a/solution.py
+++ b/solution.py
@@ -24,7 +24,7 @@
     x_v, wq_v, wkv_v, kc_v, vc_v, wo_v,
     q_all, kv_s, kv_r, qf, of, lf, part_s, part_r, att_v, term_s, term_r,
     x_sem, wq_sem, wkv_sem, kc_sem, vc_sem, wo_sem,
-    q_send, q_recv, kv_send, kv_recv, p_send, p_recv, t_send, t_recv,
+    q_send, q_relay, q_recv, kv_send, kv_recv, p_send, p_recv, t_send, t_recv,
 ):
     me = lax.axis_index("seq")
     batch, ctx_dev = kc_v.shape[0], kc_v.shape[1]
@@ -79,18 +79,26 @@
 
     pl.semaphore_wait(barrier, shards - 1)
 
-    def q_copy(slot, peer):
+    core = lax.rem(me, 2)
+    partner = me + 1 - 2 * core
+
+    def q_copy(slot, peer, sem):
         return pltpu.make_async_remote_copy(
             src_ref=q_all.at[slot], dst_ref=q_all.at[slot],
-            send_sem=q_send.at[peer], recv_sem=q_recv.at[slot],
+            send_sem=sem, recv_sem=q_recv.at[slot],
             device_id={"seq": peer}, device_id_type=MESH,
         )
 
+    def same_core(i):
+        return lax.rem(me + 2 * i, shards)
+
     def send_q(i, carry):
-        q_copy(me, lax.rem(me + i, shards)).start()
-        return carry
-
-    lax.fori_loop(1, shards, send_q, 0)
+        peer = same_core(i)
+        q_copy(me, peer, q_send.at[peer]).start()
+        return carry
+
+    lax.fori_loop(1, shards // 2, send_q, 0)
+    q_copy(me, partner, q_send.at[partner]).start()
 
     half = shards // 2
     role = me // half
@@ -140,21 +148,42 @@
     def part_local():
         return pltpu.make_async_copy(part_s.at[me], part_r.at[me], p_recv.at[me])
 
-    def attend(i, carry):
-        pair = lax.rem(my_group // PAIR + i, KV_HEADS // PAIR)
-        cols = pl.ds(pl.multiple_of(pair * PAIR * HEAD_DIM, PAIR * HEAD_DIM), PAIR * HEAD_DIM)
-        devices = PAIR * owners
-
-        def wait_q(g, c):
-            src = pair * devices + g
+    devices = PAIR * owners
+    steps = KV_HEADS // PAIR
+
+    def pair_of(i):
+        return lax.rem(my_group // PAIR + i, steps)
+
+    def relay(pair):
+        def one(g, c):
+            src = pair * devices + 2 * g + core
 
             @pl.when(src != me)
             def _():
-                q_copy(src, src).wait_recv()
+                forward = q_copy(src, partner, q_relay.at[src])
+                forward.wait_recv()
+                forward.start()
 
             return c
 
-        lax.fori_loop(0, devices, wait_q, 0)
+        lax.fori_loop(0, devices // 2, one, 0)
+
+    relay(pair_of(0))
+
+    def attend(i, carry):
+        pair = pair_of(i)
+        cols = pl.ds(pl.multiple_of(pair * PAIR * HEAD_DIM, PAIR * HEAD_DIM), PAIR * HEAD_DIM)
+
+        @pl.when(i + 1 < steps)
+        def _():
+            relay(pair_of(i + 1))
+
+        def wait_q(g, c):
+            src = pair * devices + 2 * g + 1 - core
+            q_copy(src, partner, q_relay.at[src]).wait_recv()
+            return c
+
+        lax.fori_loop(0, devices // 2, wait_q, 0)
         for g in range(devices):
             block = q_all[pair * devices + g].astype(F32)
             for h in range(heads_dev):
@@ -214,7 +243,7 @@
         lax.fori_loop(0, devices, send_part, 0)
         return carry
 
-    lax.fori_loop(0, KV_HEADS // PAIR, attend, 0)
+    lax.fori_loop(0, steps, attend, 0)
 
     owner_head = me // owners
     for r in range(2 * pieces):
@@ -235,40 +264,21 @@
     lax.fori_loop(1, shards, wait_part, 0)
     part_local().wait()
 
-    def lse_of(s, h):
-        stats = part_r[s, :, width:].astype(F32)
-        mine = (lane >= h * region) & (lane < (h + 1) * region)
-        return jnp.sum(jnp.where(mine, stats, 0.0), axis=-1, keepdims=True)
-
     new_value = jnp.concatenate([kv_r[pieces + p].astype(F32) for p in range(pieces)], axis=-1)
     new_key = jnp.concatenate([kv_r[p].astype(F32) for p in range(pieces)], axis=-1)
     own_q = q_all[me].astype(F32)
-    fresh = [
-        jnp.sum(own_q[:, h * HEAD_DIM:(h + 1) * HEAD_DIM] * new_key, axis=-1, keepdims=True) * scale
-        for h in range(heads_dev)
-    ]
-
-    def top_of(s, tops):
-        return tuple(jnp.maximum(t, lse_of(s, h)) for h, t in enumerate(tops))
-
-    tops = lax.fori_loop(0, shards, top_of, tuple(fresh))
-    shares = [jnp.exp(f - t) for f, t in zip(fresh, tops)]
-
-    def merge(s, state):
-        sums, totals = state
-        new_sums, new_totals = [], []
-        for h in range(heads_dev):
-            share = jnp.exp(lse_of(s, h) - tops[h])
-            values = part_r[s, :, h * HEAD_DIM:(h + 1) * HEAD_DIM].astype(F32)
-            new_sums.append(sums[h] + share * values)
-            new_totals.append(totals[h] + share)
-        return tuple(new_sums), tuple(new_totals)
-
-    sums, totals = lax.fori_loop(
-        0, shards, merge, (tuple(s * new_value for s in shares), tuple(shares))
-    )
+    stats = part_r[:, :, width:].astype(F32)
+    lanes = lax.broadcasted_iota(jnp.int32, stats.shape, 2)
     for h in range(heads_dev):
-        att_v[:, h * HEAD_DIM:(h + 1) * HEAD_DIM] = (sums[h] / totals[h]).astype(BF16)
+        cols = slice(h * HEAD_DIM, (h + 1) * HEAD_DIM)
+        mine = (lanes >= h * region) & (lanes < (h + 1) * region)
+        lse = jnp.sum(jnp.where(mine, stats, 0.0), axis=-1, keepdims=True)
+        fresh = jnp.sum(own_q[:, cols] * new_key, axis=-1, keepdims=True) * scale
+        top = jnp.maximum(jnp.max(lse, axis=0), fresh)
+        share = jnp.exp(lse - top[None])
+        fresh = jnp.exp(fresh - top)
+        summed = jnp.sum(share * part_r[:, :, cols].astype(F32), axis=0) + fresh * new_value
+        att_v[:, cols] = (summed / (jnp.sum(share, axis=0) + fresh)).astype(BF16)
 
     wo_copy.wait()
     out_cols = term_s.shape[2]
@@ -284,30 +294,44 @@
         cols = pl.ds(pl.multiple_of(d * out_cols, out_cols), out_cols)
         return jnp.dot(att_v[...], wo_v[:, cols], preferred_element_type=F32)
 
+    burst = 3 if (shards - 1) % 3 == 0 else 1
+
     def project(i, carry):
-        d = lax.rem(me + i, shards)
-        term_s[d] = term_of(d).astype(BF16)
-        term_copy(d, me, d).start()
-        return carry
-
-    lax.fori_loop(1, shards, project, 0)
-    own = term_of(me)
-
-    def collect(i, total):
+        targets = [lax.rem(me + 1 + i * burst + j, shards) for j in range(burst)]
+        terms = [term_of(d) for d in targets]
+        for d, term in zip(targets, terms):
+            term_s[d] = term.astype(BF16)
+        for d in targets:
+            term_copy(d, me, d).start()
+        return carry
+
+    lax.fori_loop(0, (shards - 1) // burst, project, 0)
+    term_r[me] = term_of(me).astype(BF16)
+
+    def collect(i, carry):
         s = lax.rem(me + i, shards)
         term_copy(s, s, s).wait_recv()
-        return total + term_r[s].astype(F32)
-
-    out_ref[...] = lax.fori_loop(1, shards, collect, own).astype(BF16)
+        return carry
+
+    lax.fori_loop(1, shards, collect, 0)
+    out_ref[...] = jnp.sum(term_r[...].astype(F32), axis=0).astype(BF16)
 
     def drain(i, carry):
         peer = lax.rem(me + i, shards)
-        q_copy(me, peer).wait_send()
         part_copy(peer, peer, peer).wait_send()
         term_copy(peer, peer, peer).wait_send()
         return carry
 
     lax.fori_loop(1, shards, drain, 0)
+
+    def drain_q(i, carry):
+        peer = same_core(i)
+        q_copy(me, peer, q_send.at[peer]).wait_send()
+        q_copy(peer, partner, q_relay.at[peer]).wait_send()
+        return carry
+
+    lax.fori_loop(1, shards // 2, drain_q, 0)
+    q_copy(me, partner, q_send.at[partner]).wait_send()
     for g in range(owners):
         peer = my_head * owners + g
 
@@ -353,7 +377,7 @@
             pltpu.VMEM((shards, batch, out_cols), BF16),
             pltpu.VMEM((shards, batch, out_cols), BF16),
             dma, dma((chunks,)), dma((chunks,)), dma, dma, dma,
-            dma((shards,)), dma((shards,)), dma((owners,)), dma((2 * pieces,)),
+            dma((shards,)), dma((shards,)), dma((shards,)), dma((owners,)), dma((2 * pieces,)),
             dma((shards,)), dma((shards,)), dma((shards,)), dma((shards,)),
         ],
         compiler_params=pltpu.CompilerParams(

time: 38.9 us -> 35.7 us (0.918)
  Pallas kernels: 37.3 us -> 34.2 us
    pallas_call x1, Pallas kernels: 37.3 us -> 34.2 us  [body(): pl.pallas_call(functools.partial(kernel, shards, chunks), out_shape=jax.S...]
where the time goes in v3:
time: 35.7 us; the launch traced here: 35.5 us
  Pallas kernels  34.2 us (96%)
  local copies, waits for them, and re-layouts  1.32 us (4%)
    pallas_call x1, Pallas kernels, body(): pl.pallas_call(functools.partial(kernel, shards, chunks), out_shape=jax.S...  34.2 us
    unnamed x1, local copies, waits for them, and re-layouts  1.32 us

profile of v3, /device:TPU:0, one launch (start us, length us, event | category | flops | bytes accessed | tf_op | source)
XLA Modules:
  0.0 35.5 jit_solution(12370953195959653736)
XLA Ops:
  0.0 34.2 %shard_map.73 = bf16[16,512]{1,0:T(8,128)(2,1)} custom-call(bf16[16,8192]{1,0:T(8,128)(2,1)} %x_hbm.1, bf16[8192,512]{1,0:T(8,128)(2,1)} %wq_hbm.1, bf16[8192,128]{1,0:T(8,128)(2,1)} %wkv_hbm.1, bf16[16,128,1024]{2,1,0:T(8,128)(2,1)} %kc_hbm.1, bf16[16,128,1024]{2,1,0:T(8,128)(2,1)} %vc_hbm.1, s32[16]{0:T(128)} %len_ref.1, bf16[512,8192]{1,0:T(8,128)(2,1)} %wo_hbm.1), custom_call_target="tpu_custom_call" | custom-call | tf_op jit(solution)/shard_map/pallas_call | solution.py:356
  34.2 1.3 %copy.9 = bf16[16,512]{1,0:T(8,128)(2,1)} copy(bf16[16,512]{1,0:T(8,128)(2,1)} %shard_map.73) | data formatting | bytes 32768

commit v4 on v3

--- a/solution.py
+++ b/solution.py
@@ -24,7 +24,7 @@
     x_v, wq_v, wkv_v, kc_v, vc_v, wo_v,
     q_all, kv_s, kv_r, qf, of, lf, part_s, part_r, att_v, term_s, term_r,
     x_sem, wq_sem, wkv_sem, kc_sem, vc_sem, wo_sem,
-    q_send, q_relay, q_recv, kv_send, kv_recv, p_send, p_recv, t_send, t_recv,
+    q_send, q_relay, q_recv, kv_send, kv_recv, p_send, p_recv, t_send, t_recv, h_send, h_recv, half_r,
 ):
     me = lax.axis_index("seq")
     batch, ctx_dev = kc_v.shape[0], kc_v.shape[1]
@@ -294,32 +294,53 @@
         cols = pl.ds(pl.multiple_of(d * out_cols, out_cols), out_cols)
         return jnp.dot(att_v[...], wo_v[:, cols], preferred_element_type=F32)
 
-    burst = 3 if (shards - 1) % 3 == 0 else 1
-
-    def project(i, carry):
-        targets = [lax.rem(me + 1 + i * burst + j, shards) for j in range(burst)]
+    def half_copy(d):
+        return pltpu.make_async_remote_copy(
+            src_ref=term_s.at[d], dst_ref=half_r.at[d],
+            send_sem=h_send.at[d], recv_sem=h_recv.at[d],
+            device_id={"seq": partner}, device_id_type=MESH,
+        )
+
+    burst = 4
+
+    def project_other(i, carry):
+        targets = [lax.rem(partner + 2 * (1 + i * burst + j), shards) for j in range(burst)]
         terms = [term_of(d) for d in targets]
         for d, term in zip(targets, terms):
             term_s[d] = term.astype(BF16)
         for d in targets:
-            term_copy(d, me, d).start()
-        return carry
-
-    lax.fori_loop(0, (shards - 1) // burst, project, 0)
-    term_r[me] = term_of(me).astype(BF16)
+            half_copy(d).start()
+        return carry
+
+    lax.fori_loop(0, shards // 2 // burst, project_other, 0)
+
+    def project(i, carry):
+        targets = [lax.rem(me + 2 * (1 + i * burst + j), shards) for j in range(burst)]
+        terms = [term_of(d) for d in targets]
+        for d in targets:
+            half_copy(d).wait_recv()
+        for d, term in zip(targets, terms):
+            term_s[d] = (term + half_r[d].astype(F32)).astype(BF16)
+        for d in targets:
+            @pl.when(d != me)
+            def _():
+                term_copy(d, me // 2, d).start()
+        return carry
+
+    lax.fori_loop(0, shards // 2 // burst, project, 0)
+    term_r[me // 2] = term_s[me]
 
     def collect(i, carry):
-        s = lax.rem(me + i, shards)
-        term_copy(s, s, s).wait_recv()
-        return carry
-
-    lax.fori_loop(1, shards, collect, 0)
+        s = same_core(i)
+        term_copy(s, s // 2, s).wait_recv()
+        return carry
+
+    lax.fori_loop(1, shards // 2, collect, 0)
     out_ref[...] = jnp.sum(term_r[...].astype(F32), axis=0).astype(BF16)
 
     def drain(i, carry):
         peer = lax.rem(me + i, shards)
         part_copy(peer, peer, peer).wait_send()
-        term_copy(peer, peer, peer).wait_send()
         return carry
 
     lax.fori_loop(1, shards, drain, 0)
@@ -327,10 +348,17 @@
     def drain_q(i, carry):
         peer = same_core(i)
         q_copy(me, peer, q_send.at[peer]).wait_send()
+        term_copy(peer, peer // 2, peer).wait_send()
         q_copy(peer, partner, q_relay.at[peer]).wait_send()
         return carry
 
     lax.fori_loop(1, shards // 2, drain_q, 0)
+
+    def drain_half(i, carry):
+        half_copy(lax.rem(partner + 2 * i, shards)).wait_send()
+        return carry
+
+    lax.fori_loop(0, shards // 2, drain_half, 0)
     q_copy(me, partner, q_send.at[partner]).wait_send()
     for g in range(owners):
         peer = my_head * owners + g
@@ -375,10 +403,11 @@
             pltpu.VMEM((shards, batch, width + LANES), BF16),
             pltpu.VMEM((batch, width), BF16),
             pltpu.VMEM((shards, batch, out_cols), BF16),
-            pltpu.VMEM((shards, batch, out_cols), BF16),
+            pltpu.VMEM((shards // 2, batch, out_cols), BF16),
             dma, dma((chunks,)), dma((chunks,)), dma, dma, dma,
             dma((shards,)), dma((shards,)), dma((shards,)), dma((owners,)), dma((2 * pieces,)),
             dma((shards,)), dma((shards,)), dma((shards,)), dma((shards,)),
+            dma((shards,)), dma((shards,)), pltpu.VMEM((shards, batch, out_cols), BF16),
         ],
         compiler_params=pltpu.CompilerParams(
             collective_id=0, has_side_effects=True, vmem_limit_bytes=60 * 1024 * 1024

time: 35.7 us -> 36.6 us (1.025)
  Pallas kernels: 34.2 us -> 35 us
    pallas_call x1, Pallas kernels: 34.2 us -> 35 us  [body(): pl.pallas_call(functools.partial(kernel, shards, chunks), out_shape=jax.S...]
where the time goes in v4:
time: 36.6 us; the launch traced here: 36.3 us
  Pallas kernels  35 us (96%)
  local copies, waits for them, and re-layouts  1.32 us (4%)
    pallas_call x1, Pallas kernels, body(): pl.pallas_call(functools.partial(kernel, shards, chunks), out_shape=jax.S...  35 us
    unnamed x1, local copies, waits for them, and re-layouts  1.32 us

profile of v4, /device:TPU:0, one launch (start us, length us, event | category | flops | bytes accessed | tf_op | source)
XLA Modules:
  0.0 36.3 jit_solution(3441380777715470848)
XLA Ops:
  0.0 35.0 %shard_map.73 = bf16[16,512]{1,0:T(8,128)(2,1)} custom-call(bf16[16,8192]{1,0:T(8,128)(2,1)} %x_hbm.1, bf16[8192,512]{1,0:T(8,128)(2,1)} %wq_hbm.1, bf16[8192,128]{1,0:T(8,128)(2,1)} %wkv_hbm.1, bf16[16,128,1024]{2,1,0:T(8,128)(2,1)} %kc_hbm.1, bf16[16,128,1024]{2,1,0:T(8,128)(2,1)} %vc_hbm.1, s32[16]{0:T(128)} %len_ref.1, bf16[512,8192]{1,0:T(8,128)(2,1)} %wo_hbm.1), custom_call_target="tpu_custom_call" | custom-call | tf_op jit(solution)/shard_map/pallas_call | solution.py:384
  35.0 1.3 %copy.9 = bf16[16,512]{1,0:T(8,128)(2,1)} copy(bf16[16,512]{1,0:T(8,128)(2,1)} %shard_map.73) | data formatting | bytes 32768
